TPU v7x, 32 devices: a whole 2x2x4 slice. The times are simulated.
32 devices in a mesh: mesh: 8 (over y, x, core), harm: 4 (over z).
Axes of the slice: x: 2, y: 2, z: 4, core: 2. Of those that a mesh axis runs over, the one named last changes fastest.
Arguments:
- field_in: float32 [64, 40960], P('harm', 'mesh'), may hold values from -6 to 6
- faces: int32 [2, 8192], P(None, 'mesh'), may hold values from 0 to 5119, as said below
- connectivity: int32 [6, 32768], P(None, 'mesh'), may hold values from 0 to 7167
- curl_vectors: float32 [3, 6, 32768], P(None, None, 'mesh'), may hold values from -2.4 to 2.4
- operating_point: float32 [64, 3, 8, 4096], P(None, None, None, ('mesh', 'harm')), may hold values from -2.5 to 2.5
- material: int32 [8, 4096], P(None, ('mesh', 'harm')), may hold values from 0 to 3
- bh_knots: int32 [8], replicated, may hold values from 0 to 15
- curve_base: float32 [4], replicated, may hold values from 0.5 to 2
- curve_slopes: float32 [4, 8], replicated, may hold values from 0.02 to 0.2
Outputs:
- product: float32 [64, 40960], P('harm', 'mesh')
Inputs may be any that keep to these rules, and one draw needn't show every extreme that they name: `faces`: for each partition the 1024 lower face edges and the 1024 upper face edges are 2048 distinct local edge numbers. `connectivity`: numbers below 5120 are the partition's own edges, the next 1024 the ghost edges after the upper face list of the partition below, the last 1024 those after the lower face list of the partition above.
All inputs are finite; a program needn't handle non-finite values.
Results may differ from a plain program's by a relative error of at most 0.0003.
Values sent between devices are 32-bit elements; how exact they have to be, the bound alone decides.
No kernel may reach another device: no remote copies, remote signals or barrier semaphores. Data moves between devices by JAX's collectives and lax.ppermute only.
A program may use at most 128 MiB of HBM per device.

v0:
```python
import jax
import jax.numpy as jnp
from jax import lax
from jax.sharding import PartitionSpec as P

KNOT_STEP = 0.25
KNOT_WIDTH = 0.5


def with_halo(value, sides, width):
    for axis, dim in sides:
        count, length = (lax.axis_size(axis), value.shape[dim])
        up = [(i, (i + 1) % count) for i in range(count)]
        down = [(j, i) for i, j in up]
        last = lax.slice_in_dim(value, length - width, length, axis=dim)
        first = lax.slice_in_dim(value, 0, width, axis=dim)
        before = lax.ppermute(last, axis, up)
        after = lax.ppermute(first, axis, down)
        value = jnp.concatenate([before, value, after], axis=dim)
    return value


def dft_tables(length):
    sample_idx = jnp.arange(length, dtype=jnp.int32)
    coef_idx = jnp.arange(length, dtype=jnp.int32)
    half_len = length // 2
    harmonic = jnp.where(coef_idx < half_len, coef_idx, coef_idx - half_len + 1)
    harmonic = jnp.where(coef_idx == length - 1, half_len, harmonic)
    is_sine = (coef_idx >= half_len) & (coef_idx < length - 1)
    phase_int = harmonic[:, None] * sample_idx[None, :] % length
    angles = phase_int.astype(jnp.float32) * (2.0 * jnp.pi / length)
    basis_rows = jnp.where(is_sine[:, None], jnp.sin(angles), jnp.cos(angles))
    weight = jnp.where((coef_idx == 0) | (coef_idx == length - 1), 1.0 / length, 2.0 / length)
    return (basis_rows.T, basis_rows * weight[:, None].astype(jnp.float32))


def apply_tensor(flux_step, point, material, bh_knots, curve_base, curve_slopes):
    kind_ids = jnp.arange(curve_base.shape[0], dtype=jnp.int32).reshape(
        (-1,) + (1,) * material.ndim
    )
    one_hot = (material[None] == kind_ids).astype(jnp.float32)
    base_elem = jnp.einsum("a,a...->...", curve_base, one_hot, precision=lax.Precision.HIGHEST)
    slope_elem = jnp.einsum("ak,a...->k...", curve_slopes, one_hot, precision=lax.Precision.HIGHEST)
    flux_sq = jnp.sum(point * point, axis=1)
    knot_pos = bh_knots.astype(jnp.float32) * KNOT_STEP
    scaled = (flux_sq[None] - knot_pos.reshape((-1,) + (1,) * flux_sq.ndim)) / KNOT_WIDTH
    reluct = base_elem[None] + jnp.sum(slope_elem[:, None] * jax.nn.softplus(scaled), axis=0)
    slope_sum = jnp.sum(slope_elem[:, None] * jax.nn.sigmoid(scaled), axis=0) / KNOT_WIDTH
    projected = jnp.sum(point * flux_step, axis=1)
    return reluct[:, None] * flux_step + 2.0 * (slope_sum * projected)[:, None] * point


def per_device(
    field_in,
    faces,
    connectivity,
    curl_vectors,
    operating_point,
    material,
    bh_knots,
    curve_base,
    curve_slopes,
):
    coeffs = field_in.shape[0]
    own_edges = field_in.shape[1]
    face_len = faces.shape[1]
    elements = connectivity.shape[1]
    mesh_count = lax.axis_size("mesh")
    harm_count = lax.axis_size("harm")
    block_len = operating_point.shape[3]
    samples = coeffs * harm_count
    lower_face = field_in[:, faces[0]]
    upper_face = field_in[:, faces[1]]
    padded = with_halo(jnp.concatenate([lower_face, upper_face], axis=1), (("mesh", 1),), face_len)
    extended = jnp.concatenate([field_in, padded[:, :face_len], padded[:, 3 * face_len :]], axis=1)
    gathered = extended[:, connectivity]
    curl_part = jnp.einsum("ije,cje->cie", curl_vectors, gathered, precision=lax.Precision.HIGHEST)
    arrived = lax.all_to_all(
        lax.all_to_all(
            curl_part.reshape(coeffs, 3, mesh_count, 1, harm_count, 1, block_len),
            "mesh",
            split_axis=2,
            concat_axis=3,
            tiled=True,
        ),
        "harm",
        split_axis=4,
        concat_axis=5,
        tiled=True,
    )
    arrived = arrived.reshape(coeffs, 3, mesh_count, harm_count, block_len)
    inverse, forward = dft_tables(samples)
    inverse_blocks = inverse.reshape(samples, harm_count, coeffs)
    flux_step = jnp.einsum(
        "thk,kimhe->time", inverse_blocks, arrived, precision=lax.Precision.HIGHEST
    )
    field_step = apply_tensor(
        flux_step, operating_point, material, bh_knots, curve_base, curve_slopes
    )
    forward_blocks = forward.reshape(harm_count, coeffs, samples)
    outgoing = jnp.einsum(
        "hkt,time->kimhe", forward_blocks, field_step, precision=lax.Precision.HIGHEST
    )
    returned = lax.all_to_all(
        lax.all_to_all(
            outgoing.reshape(coeffs, 3, 1, mesh_count, 1, harm_count, block_len),
            "mesh",
            split_axis=3,
            concat_axis=2,
            tiled=True,
        ),
        "harm",
        split_axis=5,
        concat_axis=4,
        tiled=True,
    )
    field_part = returned.reshape(coeffs, 3, elements)
    contrib = jnp.einsum("ije,cie->cje", curl_vectors, field_part, precision=lax.Precision.HIGHEST)
    assembled = (
        jnp.zeros((coeffs, own_edges + 2 * face_len), jnp.float32)
        .at[:, connectivity.reshape(-1)]
        .add(contrib.reshape(coeffs, -1))
    )
    ghost_sums = with_halo(assembled[:, own_edges:], (("mesh", 1),), face_len)
    result = assembled[:, :own_edges].at[:, faces[0]].add(ghost_sums[:, :face_len])
    result = result.at[:, faces[1]].add(ghost_sums[:, 3 * face_len :])
    return result


def solution(mesh):
    return jax.shard_map(
        per_device,
        mesh=mesh,
        in_specs=(
            P("harm", "mesh"),
            P(None, "mesh"),
            P(None, "mesh"),
            P(None, None, "mesh"),
            P(None, None, None, ("mesh", "harm")),
            P(None, ("mesh", "harm")),
            P(),
            P(),
            P(),
        ),
        out_specs=P("harm", "mesh"),
        check_vma=False,
    )
```

profile of v0, /device:TPU:1, one launch (start us, length us, event | category | flops | bytes accessed | tf_op | source)
XLA Modules:
  0.0 467.0 jit_solution(17183202074254305449)
XLA Ops:
  2.6 4.0 gather_fusion
  9.2 4.0 gather_fusion.1
  14.8 6.7 %copy.84 = f32[3,6,4096]{1,0,2:T(4,128)} copy(f32[3,6,4096]{2,1,0:T(8,128)} %param.12) | data formatting | bytes 589824 | tf_op args[3]
  22.9 3.1 pad_maximum_fusion
  26.0 83.9 %gather_fusion.2 = f32[24576,16]{1,0:T(8,128)} fusion(f32[16,7168]{0,1:T(8,128)} %pad_maximum_fusion, s32[24576]{0:T(1024)S(1)} %broadcast_clamp_fusion), kind=kCustom, calls=%fused_computation.2 | custom fusion | bytes 3244032 | tf_op jit(solution)/shard_map/gather | solution.py:76
  109.9 39.5 %fusion = f32[4096,16,3]{1,2,0:T(4,128)} fusion(f32[3,6,4096]{1,0,2:T(4,128)} %copy.84, f32[6,4096,16]{2,1,0:T(8,128)} %bitcast.78), kind=kOutput, calls=%fused_computation.6 | convolution fusion | flops 14155776 | bytes 2654208 | tf_op jit(solution)/shard_map/ije,cje->cie/dot_general | solution.py:77
  149.3 7.5 %copy.85 = f32[16,3,8,1,4,1,128]{6,0,4,1,5,3,2:T(8,128)} copy(f32[16,3,8,1,4,1,128]{0,1,6,4,2,5,3:T(4,128)} %bitcast.77) | data formatting | bytes 1572864 | tf_op jit(solution)/shard_map/reshape | solution.py:80
  156.8 3.6 all-to-all-start
  160.9 8.6 %all-to-all-done = f32[16,3,8,1,4,1,128]{6,0,4,1,5,3,2:T(8,128)S(1)} async-done(((f32[16,3,8,1,4,1,128]{6,0,4,1,5,3,2:T(8,128)}), f32[16,3,8,1,4,1,128]{6,0,4,1,5,3,2:T(8,128)S(1)}, u32[]{:S(2)}, u32[]{:S(2)}) %all-to-all-start) | async-done | bytes 786464 | tf_op jit(solution)/shard_map/all_to_all | solution.py:79
  170.5 4.8 %all-to-all-start.1 = ((f32[16,3,1,8,4,1,128]{6,0,3,1,5,2,4:T(8,128)}), f32[16,3,1,8,4,1,128]{6,0,3,1,5,2,4:T(8,128)S(1)}, u32[]{:S(2)}, u32[]{:S(2)}) async-start(f32[16,3,1,8,4,1,128]{6,0,3,1,5,2,4:T(8,128)} %copy.86), calls=%async_computation.1 | async-start | bytes 1572864 | tf_op jit(solution)/shard_map/all_to_all | solution.py:78
  177.5 16.0 %all-to-all-done.1 = f32[16,3,1,8,4,1,128]{6,0,3,1,5,2,4:T(8,128)S(1)} async-done(((f32[16,3,1,8,4,1,128]{6,0,3,1,5,2,4:T(8,128)}), f32[16,3,1,8,4,1,128]{6,0,3,1,5,2,4:T(8,128)S(1)}, u32[]{:S(2)}, u32[]{:S(2)}) %all-to-all-start.1) | async-done | bytes 786464 | tf_op jit(solution)/shard_map/all_to_all | solution.py:78
  197.2 7.7 %all-to-all-start.2 = ((f32[16,3,1,8,1,4,128]{6,0,5,1,4,2,3:T(8,128)}), f32[16,3,1,8,1,4,128]{6,0,5,1,4,2,3:T(8,128)S(1)}, u32[]{:S(2)}, u32[]{:S(2)}) async-start(f32[16,3,1,8,1,4,128]{6,0,5,1,4,2,3:T(8,128)} %copy.92), calls=%async_computation.2 | async-start | bytes 1572864 | tf_op jit(solution)/shard_map/all_to_all | solution.py:105
  205.0 9.0 %all-to-all-done.2 = f32[16,3,1,8,1,4,128]{6,0,5,1,4,2,3:T(8,128)S(1)} async-done(((f32[16,3,1,8,1,4,128]{6,0,5,1,4,2,3:T(8,128)}), f32[16,3,1,8,1,4,128]{6,0,5,1,4,2,3:T(8,128)S(1)}, u32[]{:S(2)}, u32[]{:S(2)}) %all-to-all-start.2) | async-done | bytes 786464 | tf_op jit(solution)/shard_map/all_to_all | solution.py:105
  215.0 3.5 all-to-all-start.3
  218.6 18.7 %all-to-all-done.3 = f32[16,3,8,1,1,4,128]{6,0,2,1,4,3,5:T(8,128)S(1)} async-done(((f32[16,3,8,1,1,4,128]{6,0,2,1,4,3,5:T(8,128)}), f32[16,3,8,1,1,4,128]{6,0,2,1,4,3,5:T(8,128)S(1)}, u32[]{:S(2)}, u32[]{:S(2)}) %all-to-all-start.3) | async-done | bytes 786464 | tf_op jit(solution)/shard_map/all_to_all | solution.py:104
  237.3 5.8 %copy.105 = f32[16,3,8,1,1,4,128]{0,1,6,5,2,4,3:T(4,128)} copy(f32[16,3,8,1,1,4,128]{6,0,2,1,4,3,5:T(8,128)S(1)} %all-to-all-done.3) | data formatting | bytes 1572864 | tf_op jit(solution)/shard_map/reshape | solution.py:117
  243.1 37.0 %convolution_bitcast_fusion = f32[16,6,4096]{0,1,2:T(8,128)} fusion(f32[16,3,4096]{0,1,2:T(4,128)} %bitcast.79, f32[3,6,4096]{1,0,2:T(4,128)} %copy.84), kind=kOutput, calls=%fused_computation.9 | convolution fusion | flops 14155776 | bytes 2654208 | tf_op jit(solution)/shard_map/ije,cie->cje/dot_general | solution.py:118
  280.2 9.6 %copy.97 = f32[16,6,4096]{2,1,0:T(8,128)S(1)} copy(f32[16,6,4096]{0,1,2:T(8,128)} %convolution_bitcast_fusion) | data formatting | bytes 3145728 | tf_op jit(solution)/shard_map/ije,cie->cje/transpose | solution.py:118
  291.9 7.6 %copy.98 = f32[24576,16]{1,0:T(8,128)} copy(f32[24576,16]{0,1:T(8,128)} %bitcast.81) | data formatting | bytes 3145728 | tf_op jit(solution)/shard_map/reshape | solution.py:122
  299.5 132.9 %scatter_custom_fusion = f32[16,7168]{0,1:T(8,128)} fusion(s32[24576]{0:T(1024)S(1)} %bitcast.86, f32[24576,16]{1,0:T(8,128)} %copy.98, f32[]{:T(128)} %constant.23.clone.1), kind=kCustom, calls=%fused_computation.16 | custom fusion | flops 393216 | bytes 459264 | tf_op jit(solution)/shard_map/scatter-add | solution.py:122
  433.9 5.3 %collective-permute-start.2 = (f32[16,1024]{0,1:T(8,128)S(1)}, f32[16,1024]{0,1:T(8,128)}, u32[]{:S(2)}, u32[]{:S(2)}) collective-permute-start(f32[16,1024]{0,1:T(8,128)S(1)} %get-tuple-element.8), channel_id=1, source_target_pairs={{0,4},{4,8},{8,12},{12,16},{16,20},{20,24},{24,28},{28,0},{1,5},{5... | collective-permute-start | bytes 196616 | tf_op jit(solution)/shard_map/ppermute | solution.py:17
  439.2 11.5 %collective-permute-done.2 = f32[16,1024]{0,1:T(8,128)} collective-permute-done((f32[16,1024]{0,1:T(8,128)S(1)}, f32[16,1024]{0,1:T(8,128)}, u32[]{:S(2)}, u32[]{:S(2)}) %collective-permute-start.2) | collective-permute-done | bytes 65568 | tf_op jit(solution)/shard_map/ppermute | solution.py:17
  450.7 7.4 %scatter_custom_fusion.1 = f32[16,5120]{0,1:T(8,128)S(1)} fusion(f32[16,5120]{0,1:T(8,128)S(1)} %slice-done, s32[1024]{0:T(1024)S(1)} %bitcast.90, f32[16,1024]{0,1:T(8,128)} %collective-permute-done.2), kind=kCustom, calls=%fused_computation.33 | custom fusion | flops 16384 | bytes 393216 | tf_op jit(solution)/shard_map/scatter-add | solution.py:125
  458.1 7.4 %scatter_custom_fusion.2 = f32[16,5120]{0,1:T(8,128)S(1)} fusion(f32[16,5120]{0,1:T(8,128)S(1)} %scatter_custom_fusion.1, s32[1024]{0:T(1024)S(1)} %bitcast.88, f32[16,1024]{0,1:T(8,128)} %collective-permute-done.3), kind=kCustom, calls=%fused_computation.31 | custom fusion | flops 16384 | bytes 393216 | tf_op jit(solution)/shard_map/scatter-add | solution.py:126
  (52 shorter events, 21.4 us)
Async XLA Ops:
  0.0 160.5 %copy-start = (f32[4,8]{1,0:T(4,128)S(1)}, f32[4,8]{1,0:T(4,128)}, u32[]{:S(2)}) copy-start(f32[4,8]{1,0:T(4,128)} %param.17) | copy-start | bytes 388
  0.0 13.2 %copy-start.3 = (s32[6,4096]{1,0:T(8,128)S(1)}, s32[6,4096]{1,0:T(8,128)}, u32[]{:S(2)}) copy-start(s32[6,4096]{1,0:T(8,128)} %param.11) | copy-start | bytes 294916
  6.6 15.0 %collective-permute-start = (f32[16,1024]{0,1:T(8,128)}, f32[16,1024]{0,1:T(8,128)S(1)}, u32[]{:S(2)}, u32[]{:S(2)}) collective-permute-start(f32[16,1024]{0,1:T(8,128)} %bitcast.91), channel_id=1, source_target_pairs={{0,4},{4,8},{8,12},{12,16},{16,20},{20,24},{24,28},{28,0},{1,5},{5... | collective-permute-start | bytes 196616 | tf_op jit(solution)/shard_map/ppermute | solution.py:17
  13.2 9.7 %collective-permute-start.1 = (f32[16,1024]{0,1:T(8,128)}, f32[16,1024]{0,1:T(8,128)}, u32[]{:S(2)}, u32[]{:S(2)}) collective-permute-start(f32[16,1024]{0,1:T(8,128)} %bitcast.92), channel_id=1, source_target_pairs={{4,0},{8,4},{12,8},{16,12},{20,16},{24,20},{28,24},{0,28},{5,1},{9... | collective-permute-start | bytes 196616 | tf_op jit(solution)/shard_map/ppermute | solution.py:18
  149.3 11.2 %copy-start.4 = (s32[8,128]{1,0:T(8,128)S(1)}, s32[8,128]{1,0:T(8,128)}, u32[]{:S(2)}) copy-start(s32[8,128]{1,0:T(8,128)} %param.14) | copy-start | bytes 12292
  149.3 11.4 %copy-start.5 = (s32[8]{0:T(128)S(1)}, s32[8]{0:T(128)}, u32[]{:S(2)}) copy-start(s32[8]{0:T(128)} %param.15) | copy-start | bytes 100
  149.3 11.4 %copy-start.6 = (f32[4]{0:T(128)S(1)}, f32[4]{0:T(128)}, u32[]{:S(2)}) copy-start(f32[4]{0:T(128)} %param.16) | copy-start | bytes 52
  156.8 18.4 %copy-start.2 = (f32[64,3,8,128]{3,2,1,0:T(8,128)S(1)}, f32[64,3,8,128]{3,2,1,0:T(8,128)}, u32[]{:S(2)}) copy-start(f32[64,3,8,128]{3,2,1,0:T(8,128)} %param.13) | copy-start | bytes 2359300
  156.8 12.6 %all-to-all-start = ((f32[16,3,8,1,4,1,128]{6,0,4,1,5,3,2:T(8,128)}), f32[16,3,8,1,4,1,128]{6,0,4,1,5,3,2:T(8,128)S(1)}, u32[]{:S(2)}, u32[]{:S(2)}) async-start(f32[16,3,8,1,4,1,128]{6,0,4,1,5,3,2:T(8,128)} %copy.85), calls=%async_computation | async-start | bytes 1572864 | tf_op jit(solution)/shard_map/all_to_all | solution.py:79
  170.5 23.0 %all-to-all-start.1 = ((f32[16,3,1,8,4,1,128]{6,0,3,1,5,2,4:T(8,128)}), f32[16,3,1,8,4,1,128]{6,0,3,1,5,2,4:T(8,128)S(1)}, u32[]{:S(2)}, u32[]{:S(2)}) async-start(f32[16,3,1,8,4,1,128]{6,0,3,1,5,2,4:T(8,128)} %copy.86), calls=%async_computation.1 | async-start | bytes 1572864 | tf_op jit(solution)/shard_map/all_to_all | solution.py:78
  197.2 16.9 %all-to-all-start.2 = ((f32[16,3,1,8,1,4,128]{6,0,5,1,4,2,3:T(8,128)}), f32[16,3,1,8,1,4,128]{6,0,5,1,4,2,3:T(8,128)S(1)}, u32[]{:S(2)}, u32[]{:S(2)}) async-start(f32[16,3,1,8,1,4,128]{6,0,5,1,4,2,3:T(8,128)} %copy.92), calls=%async_computation.2 | async-start | bytes 1572864 | tf_op jit(solution)/shard_map/all_to_all | solution.py:105
  215.0 22.3 %all-to-all-start.3 = ((f32[16,3,8,1,1,4,128]{6,0,2,1,4,3,5:T(8,128)}), f32[16,3,8,1,1,4,128]{6,0,2,1,4,3,5:T(8,128)S(1)}, u32[]{:S(2)}, u32[]{:S(2)}) async-start(f32[16,3,8,1,1,4,128]{6,0,2,1,4,3,5:T(8,128)} %copy.93), calls=%async_computation.3 | async-start | bytes 1572864 | tf_op jit(solution)/shard_map/all_to_all | solution.py:104
  432.4 18.2 %slice-start = ((f32[16,7168]{0,1:T(8,128)}), f32[16,5120]{0,1:T(8,128)S(1)}, s32[]{:S(2)}) async-start(f32[16,7168]{0,1:T(8,128)} %scatter_custom_fusion), calls=%async_computation.4 | async-start | bytes 5242880 | tf_op jit(solution)/shard_map/slice | solution.py:125
  433.9 16.8 %collective-permute-start.2 = (f32[16,1024]{0,1:T(8,128)S(1)}, f32[16,1024]{0,1:T(8,128)}, u32[]{:S(2)}, u32[]{:S(2)}) collective-permute-start(f32[16,1024]{0,1:T(8,128)S(1)} %get-tuple-element.8), channel_id=1, source_target_pairs={{0,4},{4,8},{8,12},{12,16},{16,20},{20,24},{24,28},{28,0},{1,5},{5... | collective-permute-start | bytes 196616 | tf_op jit(solution)/shard_map/ppermute | solution.py:17
  439.2 18.9 %collective-permute-start.3 = (f32[16,1024]{0,1:T(8,128)S(1)}, f32[16,1024]{0,1:T(8,128)}, u32[]{:S(2)}, u32[]{:S(2)}) collective-permute-start(f32[16,1024]{0,1:T(8,128)S(1)} %get-tuple-element.7), channel_id=1, source_target_pairs={{4,0},{8,4},{12,8},{16,12},{20,16},{24,20},{28,24},{0,28},{5,1},{9... | collective-permute-start | bytes 196616 | tf_op jit(solution)/shard_map/ppermute | solution.py:18
  450.7 16.3 %copy-start.1 = (f32[4,8]{1,0:T(4,128)S(1)}, f32[4,8]{1,0:T(4,128)}, u32[]{:S(2)}) copy-start(f32[4,8]{1,0:T(4,128)} %param.17) | copy-start | bytes 388
where the time goes:
time: 468 us; the launch traced here: 467 us
  other arithmetic  155 us (33%)
  local copies, waits for them, and re-layouts  140 us (30%)
  matrix products  79.3 us (17%)
  waiting for transfers between devices  65.2 us (14%)
  starting transfers between devices  27.6 us (6%)
    scatter-add x1, other arithmetic, per_device(): assembled = jnp.zeros((coeffs, own_edges + 2 * face_len), jnp.float32).at...  133 us
    gather x1, local copies, waits for them, and re-layouts, per_device(): gathered = extended[:, connectivity]  83.9 us
    dot_general x1, matrix products, per_device(): jnp.einsum('ije,cje->cie', curl_vectors, gathered, precision=lax.Precisio...  39.5 us
    dot_general x1, matrix products, per_device(): jnp.einsum('ije,cie->cje', curl_vectors, field_part, precision=lax.Precis...  37 us
    all_to_all x1, waiting for transfers between devices, per_device(): lax.all_to_all(lax.all_to_all(outgoing.reshape(coeffs, 3, 1, mesh_count,...  18.7 us
    all_to_all x1, waiting for transfers between devices, per_device(): lax.all_to_all(lax.all_to_all(curl_part.reshape(coeffs, 3, mesh_count, 1,...  16 us
    ppermute x2, waiting for transfers between devices, with_halo(): before = lax.ppermute(last, axis, up)  11.5 us
    unnamed x18, local copies, waits for them, and re-layouts  10.7 us
  transfers between devices with their start and end apart: 8, of which 6 were waited for; matrix products, arithmetic and copies ran while one was open for 5% of the time, Pallas kernels for 0%

commit v1 on v0

--- a/solution.py
+++ b/solution.py
@@ -75,7 +75,16 @@
     extended = jnp.concatenate([field_in, padded[:, :face_len], padded[:, 3 * face_len :]], axis=1)
     gathered = extended[:, connectivity]
     curl_part = jnp.einsum("ije,cje->cie", curl_vectors, gathered, precision=lax.Precision.HIGHEST)
-    arrived = lax.all_to_all(
+
+    def write_the_pieces_all(vals, axis_key):
+        val2 = lax.axis_size(axis_key)
+        local_out = jnp.stack(jnp.split(vals, val2, 4))
+        a_next = jnp.concatenate(
+            lax.all_to_all(local_out, axis_name=axis_key, split_axis=0, concat_axis=0), 5
+        )
+        return a_next
+
+    arrived = write_the_pieces_all(
         lax.all_to_all(
             curl_part.reshape(coeffs, 3, mesh_count, 1, harm_count, 1, block_len),
             "mesh",
@@ -84,9 +93,6 @@
             tiled=True,
         ),
         "harm",
-        split_axis=4,
-        concat_axis=5,
-        tiled=True,
     )
     arrived = arrived.reshape(coeffs, 3, mesh_count, harm_count, block_len)
     inverse, forward = dft_tables(samples)

time: 468 us -> 468 us (level)
  no operation moved by 1% of the time
where the time goes in v1:
time: 468 us; the launch traced here: 467 us
  other arithmetic  155 us (33%)
  local copies, waits for them, and re-layouts  139 us (30%)
  matrix products  79.3 us (17%)
  waiting for transfers between devices  65.2 us (14%)
  starting transfers between devices  27.6 us (6%)
    scatter-add x1, other arithmetic, per_device(): assembled = jnp.zeros((coeffs, own_edges + 2 * face_len), jnp.float32).at...  133 us
    gather x1, local copies, waits for them, and re-layouts, per_device(): gathered = extended[:, connectivity]  83.5 us
    dot_general x1, matrix products, per_device(): jnp.einsum('ije,cje->cie', curl_vectors, gathered, precision=lax.Precisio...  39.5 us
    dot_general x1, matrix products, per_device(): jnp.einsum('ije,cie->cje', curl_vectors, field_part, precision=lax.Precis...  37 us
    all_to_all x1, waiting for transfers between devices, per_device(): lax.all_to_all(lax.all_to_all(outgoing.reshape(coeffs, 3, 1, mesh_count,...  18.7 us
    all_to_all x1, waiting for transfers between devices, write_the_pieces_all(): lax.all_to_all(local_out, axis_name=axis_key, split_axis=0, concat_axis=0)  16 us
    ppermute x2, waiting for transfers between devices, with_halo(): before = lax.ppermute(last, axis, up)  11.5 us
    unnamed x18, local copies, waits for them, and re-layouts  10.7 us
  transfers between devices with their start and end apart: 8, of which 6 were waited for; matrix products, arithmetic and copies ran while one was open for 5% of the time, Pallas kernels for 0%

profile of v1, /device:TPU:1, one launch (start us, length us, event | category | flops | bytes accessed | tf_op | source)
XLA Modules:
  0.0 466.6 jit_solution(2816594935467821093)
XLA Ops:
  2.6 4.0 gather_fusion
  9.2 4.0 gather_fusion.1
  14.8 6.7 %copy.96 = f32[3,6,4096]{1,0,2:T(4,128)} copy(f32[3,6,4096]{2,1,0:T(8,128)} %param.12) | data formatting | bytes 589824 | tf_op args[3]
  22.9 3.1 pad_maximum_fusion
  25.9 83.5 %gather_fusion.2 = f32[24576,16]{1,0:T(8,128)} fusion(f32[16,7168]{0,1:T(8,128)} %pad_maximum_fusion, s32[24576]{0:T(1024)S(1)} %broadcast_clamp_fusion), kind=kCustom, calls=%fused_computation.2 | custom fusion | bytes 3244032 | tf_op jit(solution)/shard_map/gather | solution.py:76
  109.5 39.5 %fusion = f32[4096,16,3]{1,2,0:T(4,128)} fusion(f32[3,6,4096]{1,0,2:T(4,128)} %copy.96, f32[6,4096,16]{2,1,0:T(8,128)} %bitcast.94), kind=kOutput, calls=%fused_computation.6 | convolution fusion | flops 14155776 | bytes 2654208 | tf_op jit(solution)/shard_map/ije,cje->cie/dot_general | solution.py:77
  148.9 7.5 %copy.97 = f32[16,3,8,1,4,1,128]{6,0,1,4,5,3,2:T(8,128)} copy(f32[16,3,8,1,4,1,128]{0,1,6,4,2,5,3:T(4,128)} %bitcast.93) | data formatting | bytes 1572864 | tf_op jit(solution)/shard_map/reshape | solution.py:89
  156.4 3.6 all-to-all-start
  160.4 8.6 %all-to-all-done = f32[16,3,8,1,4,1,128]{6,0,1,4,5,3,2:T(8,128)S(1)} async-done(((f32[16,3,8,1,4,1,128]{6,0,1,4,5,3,2:T(8,128)}), f32[16,3,8,1,4,1,128]{6,0,1,4,5,3,2:T(8,128)S(1)}, u32[]{:S(2)}, u32[]{:S(2)}) %all-to-all-start) | async-done | bytes 786464 | tf_op jit(solution)/shard_map/all_to_all | solution.py:88
  170.1 4.8 %all-to-all-start.1 = ((f32[4,16,3,1,8,1,1,128]{7,1,4,2,6,5,3,0:T(8,128)}), f32[4,16,3,1,8,1,1,128]{7,1,4,2,6,5,3,0:T(8,128)S(1)}, u32[]{:S(2)}, u32[]{:S(2)}) async-start(f32[4,16,3,1,8,1,1,128]{7,1,4,2,6,5,3,0:T(8,128)} %copy.101), calls=%async_computation.1 | async-start | bytes 1572864 | tf_op jit(solution)/shard_map/all_to_all | solution.py:83
  177.2 16.0 %all-to-all-done.1 = f32[4,16,3,1,8,1,1,128]{7,1,4,2,6,5,3,0:T(8,128)S(1)} async-done(((f32[4,16,3,1,8,1,1,128]{7,1,4,2,6,5,3,0:T(8,128)}), f32[4,16,3,1,8,1,1,128]{7,1,4,2,6,5,3,0:T(8,128)S(1)}, u32[]{:S(2)}, u32[]{:S(2)}) %all-to-all-start.1) | async-done | bytes 786464 | tf_op jit(solution)/shard_map/all_to_all | solution.py:83
  196.9 7.7 %all-to-all-start.2 = ((f32[16,3,1,8,1,4,128]{6,0,5,1,4,2,3:T(8,128)}), f32[16,3,1,8,1,4,128]{6,0,5,1,4,2,3:T(8,128)S(1)}, u32[]{:S(2)}, u32[]{:S(2)}) async-start(f32[16,3,1,8,1,4,128]{6,0,5,1,4,2,3:T(8,128)} %copy.107), calls=%async_computation.2 | async-start | bytes 1572864 | tf_op jit(solution)/shard_map/all_to_all | solution.py:111
  204.7 9.0 %all-to-all-done.2 = f32[16,3,1,8,1,4,128]{6,0,5,1,4,2,3:T(8,128)S(1)} async-done(((f32[16,3,1,8,1,4,128]{6,0,5,1,4,2,3:T(8,128)}), f32[16,3,1,8,1,4,128]{6,0,5,1,4,2,3:T(8,128)S(1)}, u32[]{:S(2)}, u32[]{:S(2)}) %all-to-all-start.2) | async-done | bytes 786464 | tf_op jit(solution)/shard_map/all_to_all | solution.py:111
  214.7 3.5 all-to-all-start.3
  218.3 18.7 %all-to-all-done.3 = f32[16,3,8,1,1,4,128]{6,0,2,1,4,3,5:T(8,128)S(1)} async-done(((f32[16,3,8,1,1,4,128]{6,0,2,1,4,3,5:T(8,128)}), f32[16,3,8,1,1,4,128]{6,0,2,1,4,3,5:T(8,128)S(1)}, u32[]{:S(2)}, u32[]{:S(2)}) %all-to-all-start.3) | async-done | bytes 786464 | tf_op jit(solution)/shard_map/all_to_all | solution.py:110
  237.0 5.8 %copy.120 = f32[16,3,8,1,1,4,128]{0,1,6,5,2,4,3:T(4,128)} copy(f32[16,3,8,1,1,4,128]{6,0,2,1,4,3,5:T(8,128)S(1)} %all-to-all-done.3) | data formatting | bytes 1572864 | tf_op jit(solution)/shard_map/reshape | solution.py:123
  242.8 37.0 %convolution_bitcast_fusion = f32[16,6,4096]{0,1,2:T(8,128)} fusion(f32[16,3,4096]{0,1,2:T(4,128)} %bitcast.95, f32[3,6,4096]{1,0,2:T(4,128)} %copy.96), kind=kOutput, calls=%fused_computation.9 | convolution fusion | flops 14155776 | bytes 2654208 | tf_op jit(solution)/shard_map/ije,cie->cje/dot_general | solution.py:124
  279.8 9.6 %copy.112 = f32[16,6,4096]{2,1,0:T(8,128)S(1)} copy(f32[16,6,4096]{0,1,2:T(8,128)} %convolution_bitcast_fusion) | data formatting | bytes 3145728 | tf_op jit(solution)/shard_map/ije,cie->cje/transpose | solution.py:124
  291.6 7.6 %copy.113 = f32[24576,16]{1,0:T(8,128)} copy(f32[24576,16]{0,1:T(8,128)} %bitcast.97) | data formatting | bytes 3145728 | tf_op jit(solution)/shard_map/reshape | solution.py:128
  299.2 132.9 %scatter_custom_fusion = f32[16,7168]{0,1:T(8,128)} fusion(s32[24576]{0:T(1024)S(1)} %bitcast.102, f32[24576,16]{1,0:T(8,128)} %copy.113, f32[]{:T(128)} %constant.23.clone.1), kind=kCustom, calls=%fused_computation.16 | custom fusion | flops 393216 | bytes 459264 | tf_op jit(solution)/shard_map/scatter-add | solution.py:128
  433.5 5.3 %collective-permute-start.2 = (f32[16,1024]{0,1:T(8,128)S(1)}, f32[16,1024]{0,1:T(8,128)}, u32[]{:S(2)}, u32[]{:S(2)}) collective-permute-start(f32[16,1024]{0,1:T(8,128)S(1)} %get-tuple-element.8), channel_id=1, source_target_pairs={{0,4},{4,8},{8,12},{12,16},{16,20},{20,24},{24,28},{28,0},{1,5},{5... | collective-permute-start | bytes 196616 | tf_op jit(solution)/shard_map/ppermute | solution.py:17
  438.9 11.5 %collective-permute-done.2 = f32[16,1024]{0,1:T(8,128)} collective-permute-done((f32[16,1024]{0,1:T(8,128)S(1)}, f32[16,1024]{0,1:T(8,128)}, u32[]{:S(2)}, u32[]{:S(2)}) %collective-permute-start.2) | collective-permute-done | bytes 65568 | tf_op jit(solution)/shard_map/ppermute | solution.py:17
  450.4 7.4 %scatter_custom_fusion.1 = f32[16,5120]{0,1:T(8,128)S(1)} fusion(f32[16,5120]{0,1:T(8,128)S(1)} %slice-done, s32[1024]{0:T(1024)S(1)} %bitcast.106, f32[16,1024]{0,1:T(8,128)} %collective-permute-done.2), kind=kCustom, calls=%fused_computation.34 | custom fusion | flops 16384 | bytes 393216 | tf_op jit(solution)/shard_map/scatter-add | solution.py:131
  457.8 7.4 %scatter_custom_fusion.2 = f32[16,5120]{0,1:T(8,128)S(1)} fusion(f32[16,5120]{0,1:T(8,128)S(1)} %scatter_custom_fusion.1, s32[1024]{0:T(1024)S(1)} %bitcast.104, f32[16,1024]{0,1:T(8,128)} %collective-permute-done.3), kind=kCustom, calls=%fused_computation.32 | custom fusion | flops 16384 | bytes 393216 | tf_op jit(solution)/shard_map/scatter-add | solution.py:132
  (54 shorter events, 21.5 us)
Async XLA Ops:
  0.0 160.0 %copy-start = (f32[4,8]{1,0:T(4,128)S(1)}, f32[4,8]{1,0:T(4,128)}, u32[]{:S(2)}) copy-start(f32[4,8]{1,0:T(4,128)} %param.17) | copy-start | bytes 388
  0.0 13.2 %copy-start.3 = (s32[6,4096]{1,0:T(8,128)S(1)}, s32[6,4096]{1,0:T(8,128)}, u32[]{:S(2)}) copy-start(s32[6,4096]{1,0:T(8,128)} %param.11) | copy-start | bytes 294916
  6.6 14.9 %collective-permute-start = (f32[16,1024]{0,1:T(8,128)}, f32[16,1024]{0,1:T(8,128)S(1)}, u32[]{:S(2)}, u32[]{:S(2)}) collective-permute-start(f32[16,1024]{0,1:T(8,128)} %bitcast.107), channel_id=1, source_target_pairs={{0,4},{4,8},{8,12},{12,16},{16,20},{20,24},{24,28},{28,0},{1,5},{5... | collective-permute-start | bytes 196616 | tf_op jit(solution)/shard_map/ppermute | solution.py:17
  13.2 9.7 %collective-permute-start.1 = (f32[16,1024]{0,1:T(8,128)}, f32[16,1024]{0,1:T(8,128)}, u32[]{:S(2)}, u32[]{:S(2)}) collective-permute-start(f32[16,1024]{0,1:T(8,128)} %bitcast.108), channel_id=1, source_target_pairs={{4,0},{8,4},{12,8},{16,12},{20,16},{24,20},{28,24},{0,28},{5,1},{9... | collective-permute-start | bytes 196616 | tf_op jit(solution)/shard_map/ppermute | solution.py:18
  148.9 11.1 %copy-start.4 = (s32[8,128]{1,0:T(8,128)S(1)}, s32[8,128]{1,0:T(8,128)}, u32[]{:S(2)}) copy-start(s32[8,128]{1,0:T(8,128)} %param.14) | copy-start | bytes 12292
  148.9 11.4 %copy-start.5 = (s32[8]{0:T(128)S(1)}, s32[8]{0:T(128)}, u32[]{:S(2)}) copy-start(s32[8]{0:T(128)} %param.15) | copy-start | bytes 100
  148.9 11.4 %copy-start.6 = (f32[4]{0:T(128)S(1)}, f32[4]{0:T(128)}, u32[]{:S(2)}) copy-start(f32[4]{0:T(128)} %param.16) | copy-start | bytes 52
  156.4 18.6 %copy-start.2 = (f32[64,3,8,128]{3,2,1,0:T(8,128)S(1)}, f32[64,3,8,128]{3,2,1,0:T(8,128)}, u32[]{:S(2)}) copy-start(f32[64,3,8,128]{3,2,1,0:T(8,128)} %param.13) | copy-start | bytes 2359300
  156.4 12.6 %all-to-all-start = ((f32[16,3,8,1,4,1,128]{6,0,1,4,5,3,2:T(8,128)}), f32[16,3,8,1,4,1,128]{6,0,1,4,5,3,2:T(8,128)S(1)}, u32[]{:S(2)}, u32[]{:S(2)}) async-start(f32[16,3,8,1,4,1,128]{6,0,1,4,5,3,2:T(8,128)} %copy.97), calls=%async_computation | async-start | bytes 1572864 | tf_op jit(solution)/shard_map/all_to_all | solution.py:88
  170.1 23.0 %all-to-all-start.1 = ((f32[4,16,3,1,8,1,1,128]{7,1,4,2,6,5,3,0:T(8,128)}), f32[4,16,3,1,8,1,1,128]{7,1,4,2,6,5,3,0:T(8,128)S(1)}, u32[]{:S(2)}, u32[]{:S(2)}) async-start(f32[4,16,3,1,8,1,1,128]{7,1,4,2,6,5,3,0:T(8,128)} %copy.101), calls=%async_computation.1 | async-start | bytes 1572864 | tf_op jit(solution)/shard_map/all_to_all | solution.py:83
  196.9 16.9 %all-to-all-start.2 = ((f32[16,3,1,8,1,4,128]{6,0,5,1,4,2,3:T(8,128)}), f32[16,3,1,8,1,4,128]{6,0,5,1,4,2,3:T(8,128)S(1)}, u32[]{:S(2)}, u32[]{:S(2)}) async-start(f32[16,3,1,8,1,4,128]{6,0,5,1,4,2,3:T(8,128)} %copy.107), calls=%async_computation.2 | async-start | bytes 1572864 | tf_op jit(solution)/shard_map/all_to_all | solution.py:111
  214.7 22.3 %all-to-all-start.3 = ((f32[16,3,8,1,1,4,128]{6,0,2,1,4,3,5:T(8,128)}), f32[16,3,8,1,1,4,128]{6,0,2,1,4,3,5:T(8,128)S(1)}, u32[]{:S(2)}, u32[]{:S(2)}) async-start(f32[16,3,8,1,1,4,128]{6,0,2,1,4,3,5:T(8,128)} %copy.108), calls=%async_computation.3 | async-start | bytes 1572864 | tf_op jit(solution)/shard_map/all_to_all | solution.py:110
  432.1 18.2 %slice-start = ((f32[16,7168]{0,1:T(8,128)}), f32[16,5120]{0,1:T(8,128)S(1)}, s32[]{:S(2)}) async-start(f32[16,7168]{0,1:T(8,128)} %scatter_custom_fusion), calls=%async_computation.4 | async-start | bytes 5242880 | tf_op jit(solution)/shard_map/slice | solution.py:131
  433.5 16.8 %collective-permute-start.2 = (f32[16,1024]{0,1:T(8,128)S(1)}, f32[16,1024]{0,1:T(8,128)}, u32[]{:S(2)}, u32[]{:S(2)}) collective-permute-start(f32[16,1024]{0,1:T(8,128)S(1)} %get-tuple-element.8), channel_id=1, source_target_pairs={{0,4},{4,8},{8,12},{12,16},{16,20},{20,24},{24,28},{28,0},{1,5},{5... | collective-permute-start | bytes 196616 | tf_op jit(solution)/shard_map/ppermute | solution.py:17
  438.9 18.9 %collective-permute-start.3 = (f32[16,1024]{0,1:T(8,128)S(1)}, f32[16,1024]{0,1:T(8,128)}, u32[]{:S(2)}, u32[]{:S(2)}) collective-permute-start(f32[16,1024]{0,1:T(8,128)S(1)} %get-tuple-element.7), channel_id=1, source_target_pairs={{4,0},{8,4},{12,8},{16,12},{20,16},{24,20},{28,24},{0,28},{5,1},{9... | collective-permute-start | bytes 196616 | tf_op jit(solution)/shard_map/ppermute | solution.py:18
  450.4 16.3 %copy-start.1 = (f32[4,8]{1,0:T(4,128)S(1)}, f32[4,8]{1,0:T(4,128)}, u32[]{:S(2)}) copy-start(f32[4,8]{1,0:T(4,128)} %param.17) | copy-start | bytes 388
